TPU v7x, 256 devices: a whole 4x4x8 slice. The times are simulated.
256 devices in a mesh: prow: 16 (over x, y), pcol: 16 (over z, core).
Axes of the slice: x: 4, y: 4, z: 8, core: 2. Of those that a mesh axis runs over, the one named last changes fastest.
Arguments:
- matrix: float32 [16384, 16384], P('prow', 'pcol'), may hold values from -6 to 6
- pivots: int32 [2, 512], replicated, may hold values from 512 to 16383, as said below
- lower_inverses: float32 [2, 512, 512], replicated, as said below
- upper_inverses: float32 [2, 512, 512], replicated, as said below
Outputs:
- factored: float32 [16384, 16384], P('prow', 'pcol')
Inputs may be any that keep to these rules, and one draw needn't show every extreme that they name: The 512 entries of pivots[j] are distinct and each is at least (j + 1) * 512. Each lower_inverses[j] is unit lower triangular. Each upper_inverses[j] is upper triangular with a positive diagonal.
All inputs are finite; a program needn't handle non-finite values.
Results may differ from a plain program's by a relative error of at most 0.0003.
Values sent between devices are 32-bit elements; how exact they have to be, the bound alone decides.
A program may use at most 128 MiB of HBM per device.

v0:
```python
import jax
import jax.numpy as jnp
from jax import lax
from jax.sharding import PartitionSpec as P


def spread(value, axis, source):
    kept = jnp.where(lax.axis_index(axis) == source, value, 0).astype(value.dtype)
    return lax.psum(kept, axis)


def body(matrix, pivots, lower_inverses, upper_inverses):
    row_count = lax.axis_size("prow")
    col_count = lax.axis_size("pcol")
    my_row = lax.axis_index("prow")
    my_col = lax.axis_index("pcol")
    rows_local, cols_local = matrix.shape
    panel_width = lower_inverses.shape[1]
    row_blocks = jnp.arange(rows_local, dtype=jnp.int32) // panel_width * row_count + my_row
    col_blocks = jnp.arange(cols_local, dtype=jnp.int32) // panel_width * col_count + my_col
    current = matrix
    for panel_step in range(pivots.shape[0]):
        targets = pivots[panel_step]
        global_blocks = targets // panel_width
        owner_row = global_blocks % row_count
        local_slot = global_blocks // row_count * panel_width + targets % panel_width
        is_mine = owner_row == my_row
        picked = jnp.where(is_mine[:, None], current[local_slot], 0.0)
        old_top = spread(current[:panel_width], "prow", panel_step)
        inverse_lower = lower_inverses[panel_step]
        new_top = lax.psum(picked, "prow")
        formed = jnp.dot(
            inverse_lower,
            new_top,
            precision=lax.Precision.HIGHEST,
            preferred_element_type=jnp.float32,
        )
        top_rows = jnp.where((col_blocks > panel_step)[None, :], formed, new_top)
        dropped_slot = jnp.where(is_mine, local_slot, rows_local)
        current = current.at[dropped_slot].set(old_top, mode="drop")
        on_diagonal = my_row == panel_step
        current = current.at[:panel_width].set(
            jnp.where(on_diagonal, top_rows, current[:panel_width])
        )
        column = spread(current[:, :panel_width], "pcol", panel_step)
        lower_full = jnp.dot(
            column,
            upper_inverses[panel_step],
            precision=lax.Precision.HIGHEST,
            preferred_element_type=jnp.float32,
        )
        is_below = (row_blocks > panel_step)[:, None]
        lower_part = jnp.where(is_below, lower_full, 0.0)
        upper_part = jnp.where((col_blocks > panel_step)[None, :], top_rows, 0.0)
        current = current - jnp.dot(
            lower_part,
            upper_part,
            precision=lax.Precision.HIGHEST,
            preferred_element_type=jnp.float32,
        )
        current = current.at[:, :panel_width].set(
            jnp.where(is_below & (my_col == panel_step), lower_full, current[:, :panel_width])
        )
    return current


def solution(mesh):
    placed = (P("prow", "pcol"), P(), P(), P())
    return jax.shard_map(
        body, mesh=mesh, in_specs=placed, out_specs=P("prow", "pcol"), check_vma=False
    )
```

profile of v0, /device:TPU:1, one launch (start us, length us, event | category | flops | bytes accessed | tf_op | source)
XLA Modules:
  0.0 605.7 jit_solution(10775062891973166959)
XLA Ops:
  6.5 0.0 copy-start.2
  6.5 0.0 all-reduce.13.cloned.1.call-start
  6.5 4.8 copy.55
  11.3 0.0 copy-done.2
  11.5 5.8 gather_fusion
  17.3 0.0 slice-start
  17.3 3.1 copy.21
  20.3 0.0 slice-done
  20.4 1.8 copy.41
  22.2 4.8 broadcast_select_fusion.1
  27.0 0.0 all-reduce.13.cloned.1.call-update
  27.1 0.0 all-reduce.7.cloned.1.call-start
  27.2 116.5 %all-reduce.13.cloned.1.call-done = (f32[512,1024]{0,1:T(8,128)}, f32[512,1024]{0,1:T(8,128)}) async-done(((f32[512,1024]{0,1:T(8,128)}, f32[512,1024]{0,1:T(8,128)}), (f32[512,1024]{0,1:T(8,128)}, f32[512,1024]{0,1:T(8,128)})) %all-reduce.13.cloned.1.call-update) | async-done | bytes 4194320 | tf_op jit(solution)/shard_map/psum | solution.py:9
  143.7 1.9 copy.20
  145.6 6.4 %scatter_fusion = f32[1024,1024]{1,0:T(8,128)} fusion(f32[1024,1024]{1,0:T(8,128)} %copy.55, s32[512]{0:T(512)S(1)} %bitcast.54, f32[512,1024]{1,0:T(8,128)S(1)} %copy.20), kind=kCustom, calls=%fused_computation.2 | custom fusion | bytes 6293504 | tf_op jit(solution)/shard_map/scatter | solution.py:40
  152.0 5.4 copy.23
  157.4 8.1 %fusion.3 = (f32[1024,1024]{0,1:T(8,128)}, f32[512,1024]{0,1:T(8,128)S(1)}) fusion(f32[1024,1024]{0,1:T(8,128)} %copy.23, pred[]{:T(512)S(6)} %eq.59, f32[512,1024]{0,1:T(8,128)} %get-tuple-element.56, f32[2,512,512]{2,1,0:T(8,128)} %param.14, pred[1024]{0:T(1024)(128)(4,1)S(1)} %fusion.32), kind=kOutput, calls=%fused_computation.16 | convolution fusion | flops 3222274048 | bytes 11535361 | tf_op jit(solution)/shard_map/dot_general | solution.py:32
  165.5 3.2 slice_select_fusion.3
  168.7 0.0 all-reduce.7.cloned.1.call-update
  168.7 0.2 all-reduce.11.cloned.1.call-start
  168.9 0.6 compare_reduce_fusion
  169.6 114.8 %all-reduce.7.cloned.1.call-done = f32[1024,512]{0,1:T(8,128)} async-done(((f32[1024,512]{0,1:T(8,128)}), f32[1024,512]{0,1:T(8,128)}) %all-reduce.7.cloned.1.call-update) | async-done | bytes 2097168 | tf_op jit(solution)/shard_map/psum | solution.py:9
  284.3 0.0 copy-start
  284.3 5.5 fusion.11
  289.9 0.0 copy-done
  289.9 8.7 %convolution_subtract_fusion.1 = f32[1024,1024]{0,1:T(8,128)} fusion(f32[1024,1024]{0,1:T(8,128)S(1)} %copy-done, f32[512,1024]{0,1:T(8,128)S(1)} %get-tuple-element.67, f32[1024,512]{0,1:T(8,128)S(1)} %fusion.11, pred[1024]{0:T(1024)(128)(4,1)S(1)} %fusion.32, pred[1024]{0:T(1024)(128)(4,1)S(1)} %get-tuple-element.70), kind=kOutput, calls=%fused_computation.7 | convolution fusion | flops 6444548096 | bytes 12584960 | tf_op jit(solution)/shard_map/dot_general | solution.py:55
  298.6 3.9 fusion
  302.5 5.4 copy.27
  307.9 3.2 slice_select_fusion.2
  311.1 5.0 gather_fusion.1
  316.1 1.8 copy.30
  317.9 3.1 broadcast_select_fusion
  321.0 0.0 all-reduce.11.cloned.1.call-update
  321.1 0.0 all-reduce.9.cloned.1.call-start
  321.1 113.9 %all-reduce.11.cloned.1.call-done = (f32[512,1024]{0,1:T(8,128)}, f32[512,1024]{0,1:T(8,128)}) async-done(((f32[512,1024]{0,1:T(8,128)}, f32[512,1024]{0,1:T(8,128)}), (f32[512,1024]{0,1:T(8,128)}, f32[512,1024]{0,1:T(8,128)})) %all-reduce.11.cloned.1.call-update) | async-done | bytes 4194320 | tf_op jit(solution)/shard_map/psum | solution.py:9
  435.0 1.9 copy.28
  437.0 6.3 %scatter_fusion.1 = f32[1024,1024]{1,0:T(8,128)} fusion(f32[1024,1024]{1,0:T(8,128)} %copy.27, s32[512]{0:T(512)S(1)} %bitcast.55, f32[512,1024]{1,0:T(8,128)S(1)} %copy.28), kind=kCustom, calls=%fused_computation.3 | custom fusion | bytes 6293504 | tf_op jit(solution)/shard_map/scatter | solution.py:40
  443.3 5.3 copy.32
  448.6 8.0 %fusion.2 = (f32[1024,1024]{0,1:T(8,128)}, f32[512,1024]{0,1:T(8,128)S(1)}) fusion(f32[1024,1024]{0,1:T(8,128)} %copy.32, pred[]{:T(512)S(6)} %eq.64, f32[512,1024]{0,1:T(8,128)} %get-tuple-element.54, f32[2,512,512]{2,1,0:T(8,128)} %param.14, pred[1024]{0:T(1024)(128)(4,1)S(1)} %fusion.31), kind=kOutput, calls=%fused_computation.12 | convolution fusion | flops 3222274048 | bytes 11535361 | tf_op jit(solution)/shard_map/dot_general | solution.py:32
  456.7 3.2 slice_select_fusion
  459.9 0.0 all-reduce.9.cloned.1.call-update
  459.9 115.7 %all-reduce.9.cloned.1.call-done = f32[1024,512]{0,1:T(8,128)} async-done(((f32[1024,512]{0,1:T(8,128)}), f32[1024,512]{0,1:T(8,128)}) %all-reduce.9.cloned.1.call-update) | async-done | bytes 2097168 | tf_op jit(solution)/shard_map/psum | solution.py:9
  575.6 0.0 copy-start.1
  575.6 5.5 fusion.8
  581.1 0.0 copy-done.1
  581.1 8.7 %convolution_subtract_fusion = f32[1024,1024]{0,1:T(8,128)} fusion(f32[1024,1024]{0,1:T(8,128)S(1)} %copy-done.1, f32[512,1024]{0,1:T(8,128)S(1)} %get-tuple-element.69, f32[1024,512]{0,1:T(8,128)S(1)} %fusion.8, pred[1024]{0:T(1024)(128)(4,1)S(1)} %fusion.31, pred[1024]{0:T(1024)(128)(4,1)S(1)} %fusion.33), kind=kOutput, calls=%fused_computation.6 | convolution fusion | flops 6444548096 | bytes 12584960 | tf_op jit(solution)/shard_map/dot_general | solution.py:55
  589.9 3.9 fusion.1
  593.8 5.3 copy.36
  (14 shorter events, 0.2 us)
Async XLA Ops:
  6.5 4.8 copy-start.2
  6.5 137.2 %all-reduce.13.cloned.1.call-start = ((), (), s32[]{:S(2)}) async-start(), calls=%async_computation.3 | async-start | bytes 8388608 | tf_op jit(solution)/shard_map/psum | solution.py:9
  17.3 3.1 slice-start
  27.1 257.3 %all-reduce.7.cloned.1.call-start = ((), (), s32[]{:S(2)}) async-start(), calls=%async_computation | async-start | bytes 4194304 | tf_op jit(solution)/shard_map/psum | solution.py:9
  168.7 266.4 %all-reduce.11.cloned.1.call-start = ((), (), s32[]{:S(2)}) async-start(), calls=%async_computation.2 | async-start | bytes 8388608 | tf_op jit(solution)/shard_map/psum | solution.py:9
  284.3 5.5 copy-start
  321.1 254.5 %all-reduce.9.cloned.1.call-start = ((), (), s32[]{:S(2)}) async-start(), calls=%async_computation.1 | async-start | bytes 4194304 | tf_op jit(solution)/shard_map/psum | solution.py:9
  575.6 5.5 copy-start.1
Sparse Core Ops, SparseCore 0:
  27.2 116.4 all-reduce.12
  168.8 115.4 all-reduce.6
  321.2 113.8 all-reduce.10
  460.0 115.5 all-reduce.8
where the time goes:
time: 606 us
  waiting for transfers between devices  461 us (76%)
  local copies, waits for them, and re-layouts  60.3 us (10%)
  matrix products  44.6 us (7%)
  other arithmetic  26.2 us (4%)
  between operations  13.3 us (2%)
    psum x4, waiting for transfers between devices, spread(): return lax.psum(kept, axis)  461 us
    scatter x4, local copies, waits for them, and re-layouts, body(): current = current.at[dropped_slot].set(old_top, mode='drop')  23.4 us
    dot_general x2, matrix products, body(): jnp.dot(lower_part, upper_part, precision=lax.Precision.HIGHEST, preferre...  17.5 us
    dot_general x2, matrix products, body(): jnp.dot(inverse_lower, new_top, precision=lax.Precision.HIGHEST, preferre...  16.1 us
    gather x4, local copies, waits for them, and re-layouts, body(): picked = jnp.where(is_mine[:, None], current[local_slot], 0.0)  15.7 us
  transfers between devices with their start and end apart: 4, of which 4 were waited for; matrix products, arithmetic and copies ran while one was open for 0% of the time, Pallas kernels for 0%

commit v1 on v0

--- a/solution.py
+++ b/solution.py
@@ -6,7 +6,8 @@
 
 def spread(value, axis, source):
     kept = jnp.where(lax.axis_index(axis) == source, value, 0).astype(value.dtype)
-    return lax.psum(kept, axis)
+    map_play = lambda w_in, comm_axis: jnp.sum(lax.all_gather(w_in, comm_axis), axis=0)
+    return map_play(kept, axis)
 
 
 def body(matrix, pivots, lower_inverses, upper_inverses):

time: 606 us -> 1140 us (1.88)
  waiting for transfers between devices: 461 us -> 817 us
  local copies, waits for them, and re-layouts: 60.3 us -> 198 us
  other arithmetic: 26.2 us -> 60.7 us
    all_gather x0 -> x4, waiting for transfers between devices: none -> 728 us  [spread(): lax.all_gather(w_in, comm_axis)]
    psum x4 -> x2, waiting for transfers between devices: 461 us -> 89.1 us  [body(): new_top = lax.psum(picked, 'prow')]
    unnamed x8 -> x14, local copies, waits for them, and re-layouts: 6.65 us -> 144 us
    reduce_sum x0 -> x4, other arithmetic: none -> 36.7 us  [spread(): jnp.sum(lax.all_gather(w_in, comm_axis), axis=0)]
  transfers between devices with their start and end apart: 4 -> 6, of which waited for: 4 -> 6; matrix products, arithmetic and copies ran while one was open for 0% -> 13% of each run, Pallas kernels for 0% -> 0%
where the time goes in v1:
time: 1140 us; the launch traced here: 1130 us
  waiting for transfers between devices  817 us (72%)
  local copies, waits for them, and re-layouts  198 us (17%)
  other arithmetic  60.7 us (5%)
  matrix products  41.7 us (4%)
  between operations  14.2 us (1%)
    all_gather x4, waiting for transfers between devices, spread(): lax.all_gather(w_in, comm_axis)  728 us
    unnamed x14, local copies, waits for them, and re-layouts  144 us
    psum x2, waiting for transfers between devices, body(): new_top = lax.psum(picked, 'prow')  89.1 us
    reduce_sum x4, other arithmetic, spread(): jnp.sum(lax.all_gather(w_in, comm_axis), axis=0)  36.7 us
    scatter x4, local copies, waits for them, and re-layouts, body(): current = current.at[dropped_slot].set(old_top, mode='drop')  24 us
  transfers between devices with their start and end apart: 6, of which 6 were waited for; matrix products, arithmetic and copies ran while one was open for 13% of the time, Pallas kernels for 0%

profile of v1, /device:TPU:1, one launch (start us, length us, event | category | flops | bytes accessed | tf_op | source)
XLA Modules:
  0.0 1132.4 jit_solution(6810927491885352956)
XLA Ops:
  6.5 0.0 all-gather.9.cloned.1.call-start
  6.5 4.8 copy.70
  11.3 0.0 slice-start
  11.3 1.6 slice-done
  12.9 1.9 copy.56
  14.8 3.1 broadcast_select_fusion.2
  17.9 0.0 all-gather.9.cloned.1.call-update
  18.0 0.0 all-reduce.3.cloned.1.call-start
  18.0 0.6 copy-done.3
  18.7 5.0 gather_fusion
  23.7 1.8 copy.36
  25.6 3.1 broadcast_select_fusion.1
  28.7 0.0 all-reduce.3.cloned.1.call-update
  28.7 0.0 all-gather.11.cloned.1.call-start
  28.8 193.3 %all-gather.9.cloned.1.call-done = f32[8192,1024]{0,1:T(8,128)} async-done(((f32[512,1024]{0,1:T(8,128)}), f32[8192,1024]{0,1:T(8,128)}) %all-gather.9.cloned.1.call-update) | async-done | bytes 33554448 | tf_op jit(solution)/shard_map/all_gather | solution.py:9
  222.1 34.9 %copy.57 = f32[128,8,16,512]{3,2,1,0:T(8,128)S(1)} copy(f32[128,8,16,512]{3,1,2,0:T(8,128)} %bitcast.74) | data formatting | bytes 67108864
  257.0 9.7 bitcast_reduce_fusion.3
  266.7 1.9 copy.35
  268.7 6.6 scatter_fusion
  275.3 5.4 copy.38
  280.7 44.6 %all-reduce.3.cloned.1.call-done = f32[512,1024]{0,1:T(8,128)} async-done(((f32[512,1024]{0,1:T(8,128)}), f32[512,1024]{0,1:T(8,128)}) %all-reduce.3.cloned.1.call-update) | async-done | bytes 2097168 | tf_op jit(solution)/shard_map/psum | solution.py:32
  325.3 8.1 fusion.3
  333.4 3.2 slice_select_fusion.3
  336.6 0.0 all-gather.11.cloned.1.call-update
  336.6 0.0 all-gather.13.cloned.1.call-start
  336.7 0.7 compare_reduce_fusion
  337.4 175.1 %all-gather.11.cloned.1.call-done = f32[16384,512]{0,1:T(8,128)} async-done(((f32[1024,512]{0,1:T(8,128)}), f32[16384,512]{0,1:T(8,128)}) %all-gather.11.cloned.1.call-update) | async-done | bytes 33554448 | tf_op jit(solution)/shard_map/all_gather | solution.py:9
  512.5 32.5 %copy.58 = f32[64,8,16,1024]{3,2,1,0:T(8,128)S(1)} copy(f32[64,8,16,1024]{3,1,2,0:T(8,128)} %bitcast.76) | data formatting | bytes 67108864
  545.0 8.8 bitcast_reduce_fusion.2
  553.8 0.0 copy-start
  553.8 4.9 fusion.11
  558.7 0.0 copy-done
  558.7 7.0 convolution_subtract_fusion.1
  565.7 1.4 fusion
  567.1 0.0 copy-start.2
  567.1 2.0 copy-done.2
  569.1 1.7 slice_select_fusion.2
  570.8 0.0 all-gather.13.cloned.1.call-update
  570.8 0.0 all-reduce.5.cloned.1.call-start
  570.9 5.6 copy.42
  576.5 5.0 gather_fusion.1
  581.5 1.8 copy.45
  583.3 3.4 broadcast_select_fusion
  586.7 0.0 all-reduce.5.cloned.1.call-update
  586.7 0.0 all-gather.15.cloned.1.call-start
  586.8 184.1 %all-gather.13.cloned.1.call-done = f32[8192,1024]{0,1:T(8,128)} async-done(((f32[512,1024]{0,1:T(8,128)}), f32[8192,1024]{0,1:T(8,128)}) %all-gather.13.cloned.1.call-update) | async-done | bytes 33554448 | tf_op jit(solution)/shard_map/all_gather | solution.py:9
  770.9 34.9 %copy.59 = f32[128,8,16,512]{3,2,1,0:T(8,128)S(1)} copy(f32[128,8,16,512]{3,1,2,0:T(8,128)} %bitcast.75) | data formatting | bytes 67108864
  805.8 9.7 bitcast_reduce_fusion.1
  815.5 1.9 copy.43
  817.4 6.5 scatter_fusion.1
  823.9 5.5 copy.47
  829.4 44.5 %all-reduce.5.cloned.1.call-done = f32[512,1024]{0,1:T(8,128)} async-done(((f32[512,1024]{0,1:T(8,128)}), f32[512,1024]{0,1:T(8,128)}) %all-reduce.5.cloned.1.call-update) | async-done | bytes 2097168 | tf_op jit(solution)/shard_map/psum | solution.py:32
  873.9 8.0 fusion.2
  881.9 3.2 slice_select_fusion
  885.2 0.0 all-gather.15.cloned.1.call-update
  885.2 175.8 %all-gather.15.cloned.1.call-done = f32[16384,512]{0,1:T(8,128)} async-done(((f32[1024,512]{0,1:T(8,128)}), f32[16384,512]{0,1:T(8,128)}) %all-gather.15.cloned.1.call-update) | async-done | bytes 33554448 | tf_op jit(solution)/shard_map/all_gather | solution.py:9
  1061.0 32.5 %copy.60 = f32[64,8,16,1024]{3,2,1,0:T(8,128)S(1)} copy(f32[64,8,16,1024]{3,1,2,0:T(8,128)} %bitcast.77) | data formatting | bytes 67108864
  1093.5 8.6 bitcast_reduce_fusion
  1102.2 0.0 copy-start.1
  1102.2 4.9 fusion.8
  1107.1 0.0 copy-done.1
  1107.1 8.7 convolution_subtract_fusion
  1115.8 4.0 fusion.1
  1119.8 5.3 copy.51
  (16 shorter events, 0.2 us)
Async XLA Ops:
  6.5 215.6 %all-gather.9.cloned.1.call-start = ((), (), s32[]{:S(2)}) async-start(), calls=%async_computation.2 | async-start | bytes 35651584 | tf_op jit(solution)/shard_map/all_gather | solution.py:9
  11.3 1.6 slice-start
  17.9 0.7 copy-start.3
  18.0 307.3 %all-reduce.3.cloned.1.call-start = ((), (), s32[]{:S(2)}) async-start(), calls=%async_computation | async-start | bytes 4194304 | tf_op jit(solution)/shard_map/psum | solution.py:32
  28.7 483.7 %all-gather.11.cloned.1.call-start = ((), (), s32[]{:S(2)}) async-start(), calls=%async_computation.3 | async-start | bytes 35651584 | tf_op jit(solution)/shard_map/all_gather | solution.py:9
  336.6 434.3 %all-gather.13.cloned.1.call-start = ((), (), s32[]{:S(2)}) async-start(), calls=%async_computation.4 | async-start | bytes 35651584 | tf_op jit(solution)/shard_map/all_gather | solution.py:9
  553.8 4.9 copy-start
  567.1 2.0 copy-start.2
  570.8 303.1 %all-reduce.5.cloned.1.call-start = ((), (), s32[]{:S(2)}) async-start(), calls=%async_computation.1 | async-start | bytes 4194304 | tf_op jit(solution)/shard_map/psum | solution.py:32
  586.7 474.3 %all-gather.15.cloned.1.call-start = ((), (), s32[]{:S(2)}) async-start(), calls=%async_computation.5 | async-start | bytes 35651584 | tf_op jit(solution)/shard_map/all_gather | solution.py:9
  1102.2 4.9 copy-start.1
Sparse Core Ops, SparseCore 0:
  18.1 204.0 all-gather.8
  225.4 99.7 all-reduce.2
  336.8 175.6 all-gather.10
  570.9 199.9 all-gather.12
  774.1 99.7 all-reduce.4
  885.3 175.6 all-gather.14
